TPU v7x, 32 devices: a whole 2x2x4 slice. The times are simulated.
32 devices in a mesh: dp: 8 (over y, x, core), group: 4 (over z).
Axes of the slice: x: 2, y: 2, z: 4, core: 2. Of those that a mesh axis runs over, the one named last changes fastest.
Arguments:
- images: bfloat16 [4096, 512], P(('dp', 'group')), may hold values from -1 to 1
- texts: bfloat16 [4096, 512], P(('dp', 'group')), may hold values from -1 to 1
- log_scale: float32 [], replicated, may hold values from 2 to 2.7
Outputs:
- grad_images: bfloat16 [4096, 512], P(('dp', 'group'))
- grad_texts: bfloat16 [4096, 512], P(('dp', 'group'))
- loss: float32 [], replicated
- grad_scale: float32 [], replicated
All inputs are finite; a program needn't handle non-finite values.
Results may differ from a plain program's by a relative error of at most 0.0013.
The roundings to bfloat16 on the way count: a program that leaves them out, or rounds other values in their place, can miss the bound.
Values may be sent and summed in bfloat16 or wider, within the bound.
A program may use at most 128 MiB of HBM per device.

v0:
```python
import jax
import jax.numpy as jnp
from jax import lax
from jax.sharding import PartitionSpec as P


def body(images, texts, log_scale):
    row_count = images.shape[0]
    device_count = lax.axis_size(("dp", "group"))
    pair_total = row_count * device_count
    within = lax.all_gather(texts, "group", axis=0, tiled=True)
    texts_whole = lax.all_gather(within, "dp", axis=0, tiled=True)
    images_whole = lax.all_gather(images, ("dp", "group"), axis=0, tiled=True)
    logit_scale = jnp.exp(log_scale)
    first_pair = lax.axis_index(("dp", "group")) * row_count
    contract_last = (((1,), (1,)), ((), ()))
    contract_first = (((0,), (0,)), ((), ()))
    row_logits = logit_scale * lax.dot_general(
        images, texts_whole, contract_last, preferred_element_type=jnp.float32
    )
    row_top = jnp.max(row_logits, axis=1)
    row_lse = row_top + jnp.log(jnp.sum(jnp.exp(row_logits - row_top[:, None]), axis=1))
    paired = jnp.diagonal(lax.dynamic_slice_in_dim(row_logits, first_pair, row_count, 1))
    part_top = jnp.max(row_logits, axis=0)
    part_sum = jnp.sum(jnp.exp(row_logits - part_top[None, :]), axis=0)
    got_top, got_sum = (
        lax.all_to_all(
            part_top.reshape(device_count, row_count),
            ("dp", "group"),
            split_axis=0,
            concat_axis=0,
            tiled=True,
        ),
        lax.all_to_all(
            part_sum.reshape(device_count, row_count),
            ("dp", "group"),
            split_axis=0,
            concat_axis=0,
            tiled=True,
        ),
    )
    col_top = jnp.max(got_top, axis=0)
    col_lse = col_top + jnp.log(jnp.sum(got_sum * jnp.exp(got_top - col_top[None, :]), axis=0))
    row_whole, col_whole = (
        lax.all_gather(row_lse, ("dp", "group"), axis=0, tiled=True),
        lax.all_gather(col_lse, ("dp", "group"), axis=0, tiled=True),
    )
    own_pairs = (
        jnp.arange(pair_total)[None, :] == (first_pair + jnp.arange(row_count))[:, None]
    ).astype(jnp.float32)
    row_grad = (
        0.5 * (jnp.exp(row_logits - row_lse[:, None]) + jnp.exp(row_logits - col_whole[None, :]))
        - own_pairs
    )
    scale_part = jnp.sum(row_grad * row_logits)
    row_weights = row_grad.astype(jnp.bfloat16)
    grad_images = (
        logit_scale * jnp.dot(row_weights, texts_whole, preferred_element_type=jnp.float32)
    ).astype(jnp.bfloat16)
    col_logits = logit_scale * lax.dot_general(
        images_whole, texts, contract_last, preferred_element_type=jnp.float32
    )
    col_grad = (
        0.5 * (jnp.exp(col_logits - row_whole[:, None]) + jnp.exp(col_logits - col_lse[None, :]))
        - own_pairs.T
    )
    text_sum = logit_scale * lax.dot_general(
        col_grad.astype(jnp.bfloat16),
        images_whole,
        contract_first,
        preferred_element_type=jnp.float32,
    )
    grad_texts = text_sum.astype(jnp.bfloat16)
    loss_part = jnp.sum(row_lse) + jnp.sum(col_lse) - 2.0 * jnp.sum(paired)
    loss_total, scale_total = lax.psum((loss_part, scale_part), ("dp", "group"))
    return (grad_images, grad_texts, loss_total / (2.0 * pair_total), scale_total / pair_total)


def solution(mesh):
    in_specs = (P(("dp", "group"), None), P(("dp", "group"), None), P())
    out_specs = (P(("dp", "group"), None), P(("dp", "group"), None), P(), P())
    return jax.shard_map(body, mesh=mesh, in_specs=in_specs, out_specs=out_specs, check_vma=False)
```

profile of v0, /device:TPU:0, one launch (start us, length us, event | category | flops | bytes accessed | tf_op | source)
XLA Modules:
  0.0 281.2 jit_solution(1704532022172781684)
XLA Ops:
  7.2 0.0 all-gather.5.cloned.1.call-start
  7.2 19.3 %all_gather.15 = bf16[512,512]{1,0:T(8,128)(2,1)} all-gather(bf16[128,512]{1,0:T(8,128)(2,1)} %param.4), channel_id=1, replica_groups=mesh['dp'=8,'group'=4] {'group'}, dimensions={0}, use_global_device_ids=true | all-gather | bytes 655360 | tf_op jit(solution)/shard_map/all_gather | solution.py:11
  26.5 0.0 all-gather.5.cloned.1.call-update
  26.6 0.0 all-gather.7.cloned.1.call-start
  26.6 0.7 all-gather.7.cloned.1.call-update
  28.0 35.0 %all-gather.5.cloned.1.call-done = bf16[4096,512]{1,0:T(8,128)(2,1)} async-done(((bf16[512,512]{1,0:T(8,128)(2,1)}), bf16[4096,512]{1,0:T(8,128)(2,1)}) %all-gather.5.cloned.1.call-update) | async-done | bytes 4194320 | tf_op jit(solution)/shard_map/all_gather | solution.py:12
  63.1 4.4 %fusion.10 = (f32[128]{0:T(128)S(1)}, f32[4096]{0:T(1024)}, f32[128,4096]{1,0:T(8,128)S(1)}) fusion(bf16[128,512]{1,0:T(8,128)(2,1)} %param.3, bf16[4096,512]{1,0:T(8,128)(2,1)} %all-gather.5.cloned.1.call-done, f32[]{:T(128)S(6)} %exp.24), kind=kOutput, calls=%fused_computation.27 | convolution fusion | flops 538439552 | bytes 6439428 | tf_op jit(solution)/shard_map/dot_general | solution.py:18
  67.5 4.6 %all-to-all-start = ((f32[32,1,128]{2,1,0:T(1,128)}), f32[32,1,128]{2,1,0:T(1,128)S(1)}, u32[]{:S(2)}, u32[]{:S(2)}) async-start(f32[32,1,128]{2,1,0:T(1,128)} %bitcast), calls=%async_computation | async-start | bytes 32768 | tf_op jit(solution)/shard_map/all_to_all | solution.py:27
  72.1 2.0 exponential_reduce_fusion.1
  74.2 0.6 fusion.12
  74.8 4.5 %all-to-all-done = f32[32,1,128]{2,1,0:T(1,128)S(1)} async-done(((f32[32,1,128]{2,1,0:T(1,128)}), f32[32,1,128]{2,1,0:T(1,128)S(1)}, u32[]{:S(2)}, u32[]{:S(2)}) %all-to-all-start) | async-done | bytes 16416 | tf_op jit(solution)/shard_map/all_to_all | solution.py:27
  79.2 2.5 all-to-all-start.1
  81.8 1.2 gather_fusion
  83.1 0.6 reduce_sum.68
  84.3 0.1 reduce_max.29
  84.4 4.6 %all-to-all-done.1 = f32[32,1,128]{2,1,0:T(1,128)S(1)} async-done(((f32[32,1,128]{2,1,0:T(1,128)}), f32[32,1,128]{2,1,0:T(1,128)S(1)}, u32[]{:S(2)}, u32[]{:S(2)}) %all-to-all-start.1) | async-done | bytes 16416 | tf_op jit(solution)/shard_map/all_to_all | solution.py:34
  89.0 0.6 fusion.11
  90.9 64.1 %all-gather = f32[32,1,128]{2,1,0:T(1,128)S(1)} all-gather(f32[1,1,128]{2,1,0:T(1,128)S(1)} %bitcast.22), channel_id=1, replica_groups=mesh['dp'=8,'group'=4] {'dp','group'}, dimensions={0}, use_global_device_ids=true | all-gather | bytes 16896 | tf_op jit(solution)/shard_map/all_gather | solution.py:46
  155.0 1.5 multiply_reduce_fusion
  156.5 65.1 %all-gather.1 = f32[32,1,128]{2,1,0:T(1,128)S(1)} all-gather(f32[1,1,128]{2,1,0:T(1,128)S(1)} %bitcast.21), channel_id=1, replica_groups=mesh['dp'=8,'group'=4] {'dp','group'}, dimensions={0}, use_global_device_ids=true | all-gather | bytes 16896 | tf_op jit(solution)/shard_map/all_gather | solution.py:45
  221.6 38.4 %all-reduce = (f32[]{:T(128)}, f32[]{:T(128)}) all-reduce(f32[]{:T(128)S(6)} %sub.81, f32[]{:T(128)} %multiply_reduce_fusion), channel_id=1, replica_groups=mesh['dp'=8,'group'=4] {'dp','group'}, use_global_device_ids=true, to_apply=%region_9.10 | all-reduce | flops 2 | bytes 16 | tf_op jit(solution)/shard_map/psum | solution.py:75
  261.4 0.0 copy-start
  261.4 4.0 %fusion.1 = bf16[128,512]{1,0:T(8,128)(2,1)} fusion(bf16[4096,512]{1,0:T(8,128)(2,1)} %all-gather.5.cloned.1.call-done, f32[128,4096]{1,0:T(8,128)S(1)} %get-tuple-element.14, s32[128]{0:T(128)S(1)} %iota_add_fusion, f32[4096]{0:T(1024)S(1)} %bitcast.18, f32[128]{0:T(128)S(1)} %get-tuple-element.13, f32[]{:T(128)S(6)} %exp.24), kind=kOutput, calls=%fused_computation.13 | convolution fusion | flops 541196288 | bytes 6439940 | tf_op jit(solution)/shard_map/dot_general | solution.py:58
  265.4 0.0 all-gather.7.cloned.1.call-done
  265.4 0.0 copy-done
  265.4 6.7 %fusion.2 = bf16[128,512]{1,0:T(8,128)(2,1)} fusion(bf16[4096,512]{1,0:T(8,128)(2,1)} %all-gather.7.cloned.1.call-done, bf16[128,512]{1,0:T(8,128)(2,1)S(1)} %copy-done, s32[128]{0:T(128)S(1)} %iota_add_fusion, f32[128]{0:T(128)S(1)} %get-tuple-element.11, f32[4096]{0:T(1024)S(1)} %bitcast.20, f32[]{:T(128)S(6)} %exp.24), kind=kOutput, calls=%fused_computation.14 | convolution fusion | flops 1078591488 | bytes 4473860 | tf_op jit(solution)/shard_map/dot_general | solution.py:67
  (4 shorter events, 0.1 us)
Async XLA Ops:
  7.2 55.9 %all-gather.5.cloned.1.call-start = ((), (), s32[]{:S(2)}) async-start(), calls=%async_computation.2 | async-start | bytes 4718592 | tf_op jit(solution)/shard_map/all_gather | solution.py:12
  26.6 238.8 %all-gather.7.cloned.1.call-start = ((), (), s32[]{:S(2)}) async-start(), calls=%async_computation.3 | async-start | bytes 4325376 | tf_op jit(solution)/shard_map/all_gather | solution.py:13
  67.5 11.7 %all-to-all-start = ((f32[32,1,128]{2,1,0:T(1,128)}), f32[32,1,128]{2,1,0:T(1,128)S(1)}, u32[]{:S(2)}, u32[]{:S(2)}) async-start(f32[32,1,128]{2,1,0:T(1,128)} %bitcast), calls=%async_computation | async-start | bytes 32768 | tf_op jit(solution)/shard_map/all_to_all | solution.py:27
  79.2 9.7 %all-to-all-start.1 = ((f32[32,1,128]{2,1,0:T(1,128)}), f32[32,1,128]{2,1,0:T(1,128)S(1)}, u32[]{:S(2)}, u32[]{:S(2)}) async-start(f32[32,1,128]{2,1,0:T(1,128)} %bitcast.1), calls=%async_computation.1 | async-start | bytes 32768 | tf_op jit(solution)/shard_map/all_to_all | solution.py:34
  261.4 4.0 %copy-start = (bf16[128,512]{1,0:T(8,128)(2,1)S(1)}, bf16[128,512]{1,0:T(8,128)(2,1)}, u32[]{:S(2)}) copy-start(bf16[128,512]{1,0:T(8,128)(2,1)} %param.4) | copy-start | bytes 393220
Sparse Core Ops, SparseCore 0:
  26.7 36.3 all-gather.4
  66.1 61.6 all-gather.6
where the time goes:
time: 282 us; the launch traced here: 281 us
  blocking collectives  187 us (66%)
  waiting for transfers between devices  44.8 us (16%)
  between operations  20.3 us (7%)
  matrix products  15.1 us (5%)
  starting transfers between devices  7.21 us (3%)
  other arithmetic  5.48 us (2%)
    all_gather x1, blocking collectives, body(): lax.all_gather(row_lse, ('dp', 'group'), axis=0, tiled=True)  65.1 us
    all_gather x1, blocking collectives, body(): lax.all_gather(col_lse, ('dp', 'group'), axis=0, tiled=True)  64.1 us
    psum x1, blocking collectives, body(): loss_total, scale_total = lax.psum((loss_part, scale_part), ('dp', 'group'))  38.4 us
    all_gather x1, waiting for transfers between devices, body(): texts_whole = lax.all_gather(within, 'dp', axis=0, tiled=True)  35 us
    all_gather x1, blocking collectives, body(): within = lax.all_gather(texts, 'group', axis=0, tiled=True)  19.3 us
    dot_general x1, matrix products, body(): lax.dot_general(col_grad.astype(jnp.bfloat16), images_whole, contract_fir...  6.7 us
  transfers between devices with their start and end apart: 4, of which 3 were waited for; matrix products, arithmetic and copies ran while one was open for 5% of the time, Pallas kernels for 0%

commit v1 on v0

v1 whole, which is shorter than its diff:
```python
import functools

import jax
import jax.numpy as jnp
from jax import lax
from jax.experimental import pallas as pl
from jax.experimental.pallas import tpu as pltpu
from jax.sharding import PartitionSpec as P

MESH = pl.DeviceIdType.MESH
NT = (((1,), (1,)), ((), ()))
NN = (((1,), (0,)), ((), ()))
TN = (((0,), (0,)), ((), ()))
F32 = jnp.float32
BLOCK, STAT, GRAD, SCALAR = range(4)


def each(count, step):
    if count <= 8:
        for i in range(count):
            step(i)
    else:
        lax.fori_loop(0, count, lambda i, c: (step(i), c)[1], 0)


def kernel(
    gn, dn, images, texts, log_scale, gi_out, gt_out, loss_out, scale_out,
    img_all, txt_all, logits, weights, row_stat, col_stat, top, acc, row_lse, col_lse,
    gi_send, gi_recv, gt_send, gt_recv, sc_group, sc_dp, g_send, g_recv, d_send, d_recv,
):
    rows, width = images.shape
    g = lax.axis_index("group")
    d = lax.axis_index("dp")
    wide = 2 * rows if dn % 2 == 0 else rows
    per = wide // rows
    chunks = dn // per

    def g_peer(o):
        return lax.rem(g + o, gn)

    def d_peer(o):
        return lax.rem(d + o, dn)

    def at(k, n=rows):
        return pl.ds(pl.multiple_of(k * n, n), n)

    def g_copy(kind, src, dst, to, slot):
        return pltpu.make_async_remote_copy(
            src_ref=src, dst_ref=dst, send_sem=g_send.at[kind, to], recv_sem=g_recv.at[kind, slot],
            device_id={"group": to}, device_id_type=MESH)

    def d_copy(kind, src, dst, to, slot):
        return pltpu.make_async_remote_copy(
            src_ref=src, dst_ref=dst, send_sem=d_send.at[kind, to], recv_sem=d_recv.at[kind, slot],
            device_id={"dp": to}, device_id_type=MESH)

    barrier = pltpu.get_barrier_semaphore()
    each(gn - 1, lambda i: pl.semaphore_signal(
        barrier, inc=1, device_id={"group": g_peer(i + 1)}, device_id_type=MESH))
    each(dn - 1, lambda i: pl.semaphore_signal(
        barrier, inc=1, device_id={"dp": d_peer(i + 1)}, device_id_type=MESH))
    pl.semaphore_wait(barrier, gn + dn - 2)

    each(gn - 1, lambda i: g_copy(BLOCK, images, img_all.at[at(g)], g_peer(i + 1), g).start())
    each(dn - 1, lambda i: d_copy(BLOCK, texts, txt_all.at[at(d)], d_peer(i + 1), d).start())
    img_all[at(g), :] = images[...]
    txt_all[at(d), :] = texts[...]
    s = jnp.exp(log_scale[...])
    eye = (lax.broadcasted_iota(jnp.int32, (rows, rows), 0)
           == lax.broadcasted_iota(jnp.int32, (rows, rows), 1))

    def wait_image(i):
        k = g_peer(i + 1)
        g_copy(BLOCK, images, img_all.at[at(k)], k, k).wait_recv()

    each(gn - 1, wait_image)

    def logits_chunk(i):
        c = lax.rem(d // per + i, chunks)

        def wait_text(j):
            k = c * per + j

            @pl.when(k != d)
            def _():
                d_copy(BLOCK, texts, txt_all.at[at(k)], k, k).wait_recv()

        each(per, wait_text)
        part = s * lax.dot_general(img_all[...], txt_all[at(c, wide), :], NT, preferred_element_type=F32)
        logits[:, at(c, wide)] = part
        high = jnp.max(part, axis=0, keepdims=True)
        col_stat[d, 0:1, at(c, wide)] = high
        col_stat[d, 1:2, at(c, wide)] = jnp.sum(jnp.exp(part - high), axis=0, keepdims=True)
        if isinstance(i, int) and i == 0:
            top[...] = part
        else:
            top[...] = jnp.maximum(top[...], part)

    if chunks > 8:
        top[...] = jnp.full(top.shape, -jnp.inf, F32)
    each(chunks, logits_chunk)
    each(dn - 1, lambda i: d_copy(STAT, col_stat.at[d], col_stat.at[d], d_peer(i + 1), d).start())

    def flat(col):
        return jnp.sum(jnp.where(eye, col, 0.0), axis=0, keepdims=True)

    def stand(line):
        return jnp.sum(jnp.where(eye, line, 0.0), axis=1, keepdims=True)

    for k in range(gn):
        band = pl.ds(k * rows, rows)
        high = jnp.max(top[band, :], axis=1, keepdims=True)
        acc[...] = jnp.zeros(acc.shape, F32)

        def add(c):
            acc[...] += jnp.exp(logits[band, at(c, wide)] - high)

        each(chunks, add)
        row_stat[g, 0:1, band] = flat(high)
        row_stat[g, 1:2, band] = flat(jnp.sum(acc[...], axis=1, keepdims=True))
    each(gn - 1, lambda i: g_copy(STAT, row_stat.at[g], row_stat.at[g], g_peer(i + 1), g).start())

    def wait_row(i):
        k = g_peer(i + 1)
        g_copy(STAT, row_stat.at[k], row_stat.at[k], k, k).wait_recv()

    def wait_col(i):
        k = d_peer(i + 1)
        d_copy(STAT, col_stat.at[k], col_stat.at[k], k, k).wait_recv()

    def lse(stat):
        high = jnp.max(stat[:, 0, :], axis=0, keepdims=True)
        return high + jnp.log(jnp.sum(stat[:, 1, :] * jnp.exp(stat[:, 0, :] - high), axis=0, keepdims=True))

    each(dn - 1, wait_col)
    col_lse[...] = lse(col_stat)
    each(gn - 1, wait_row)
    row_lse[...] = lse(row_stat)

    acc[...] = jnp.zeros(acc.shape, F32)
    step_of = (lax.broadcasted_iota(jnp.int32, (rows, wide), 1)
               - lax.broadcasted_iota(jnp.int32, (rows, wide), 0))
    for o in [*range(1, gn), 0]:
        k = g_peer(o)
        line = stand(row_lse[0:1, at(k)])

        def weigh(c):
            part = logits[at(k), at(c, wide)]
            w = 0.5 * (jnp.exp(part - line) + jnp.exp(part - col_lse[0:1, at(c, wide)]))
            if o == 0:
                w = w - jnp.where(step_of == d * rows - c * wide, 1.0, 0.0)
            acc[...] += w * part
            weights[at(k), at(c, wide)] = w.astype(jnp.bfloat16)

        each(chunks, weigh)
        gi_send[k] = lax.dot_general(weights[at(k), :], txt_all[...], NN, preferred_element_type=F32)
        if o:
            g_copy(GRAD, gi_send.at[k], gi_recv.at[g], k, g).start()

    own = logits[at(g), at(d)]
    pairs = jnp.sum(jnp.where(eye, own, 0.0), axis=0, keepdims=True)
    loss_part = jnp.sum(row_lse[0:1, at(g)] + col_lse[0:1, at(d)] - 2.0 * pairs, axis=1, keepdims=True)
    scale_part = jnp.sum(jnp.sum(acc[...], axis=0, keepdims=True), axis=1, keepdims=True)
    first = lax.broadcasted_iota(jnp.int32, (8, 128), 1) == 0
    sc_group[g] = jnp.where(first, loss_part, scale_part)
    each(gn - 1, lambda i: g_copy(SCALAR, sc_group.at[g], sc_group.at[g], g_peer(i + 1), g).start())

    def text_chunk(i):
        c = lax.rem(d // per + 1 + i, chunks)
        part = lax.dot_general(weights[:, at(c, wide)], img_all[...], TN, preferred_element_type=F32)
        for j in range(per):
            k = c * per + j
            gt_send[k] = part[j * rows:(j + 1) * rows]

            @pl.when(k != d)
            def _():
                d_copy(GRAD, gt_send.at[k], gt_recv.at[d], k, d).start()

    each(chunks, text_chunk)

    def wait_sc_group(i):
        k = g_peer(i + 1)
        g_copy(SCALAR, sc_group.at[k], sc_group.at[k], k, k).wait_recv()

    each(gn - 1, wait_sc_group)
    sc_dp[d] = jnp.sum(sc_group[...], axis=0)
    each(dn - 1, lambda i: d_copy(SCALAR, sc_dp.at[d], sc_dp.at[d], d_peer(i + 1), d).start())

    def take_g(i):
        k = g_peer(i + 1)
        g_copy(GRAD, gi_send.at[k], gi_recv.at[k], k, k).wait_recv()
        gi_send[g] += gi_recv[k]

    def take_d(i):
        k = d_peer(i + 1)
        d_copy(GRAD, gt_send.at[k], gt_recv.at[k], k, k).wait_recv()
        gt_send[d] += gt_recv[k]

    each(gn - 1, take_g)
    gi_out[...] = (s * gi_send[g]).astype(gi_out.dtype)
    each(dn - 1, take_d)
    gt_out[...] = (s * gt_send[d]).astype(gt_out.dtype)

    def wait_sc_dp(i):
        k = d_peer(i + 1)
        d_copy(SCALAR, sc_dp.at[k], sc_dp.at[k], k, k).wait_recv()

    each(dn - 1, wait_sc_dp)
    total = jnp.sum(sc_dp[...], axis=0)
    pair_total = gn * dn * rows
    loss_out[...] = total[0:1, 0:1] / (2.0 * pair_total)
    scale_out[...] = total[0:1, 1:2] / pair_total

    def end_g(i):
        k = g_peer(i + 1)
        g_copy(BLOCK, images, img_all.at[at(g)], k, g).wait_send()
        g_copy(STAT, row_stat.at[g], row_stat.at[g], k, g).wait_send()
        g_copy(GRAD, gi_send.at[k], gi_recv.at[g], k, g).wait_send()
        g_copy(SCALAR, sc_group.at[g], sc_group.at[g], k, g).wait_send()

    def end_d(i):
        k = d_peer(i + 1)
        d_copy(BLOCK, texts, txt_all.at[at(d)], k, d).wait_send()
        d_copy(STAT, col_stat.at[d], col_stat.at[d], k, d).wait_send()
        d_copy(GRAD, gt_send.at[k], gt_recv.at[d], k, d).wait_send()
        d_copy(SCALAR, sc_dp.at[d], sc_dp.at[d], k, d).wait_send()

    each(gn - 1, end_g)
    each(dn - 1, end_d)


def body(gn, dn, images, texts, log_scale):
    rows, width = images.shape
    high, across = gn * rows, dn * rows
    wide = 2 * rows if dn % 2 == 0 else rows
    vmem = pl.BlockSpec(memory_space=pltpu.VMEM)
    gi, gt, loss, scale = pl.pallas_call(
        functools.partial(kernel, gn, dn),
        out_shape=(
            jax.ShapeDtypeStruct(images.shape, images.dtype),
            jax.ShapeDtypeStruct(texts.shape, texts.dtype),
            jax.ShapeDtypeStruct((1, 1), F32),
            jax.ShapeDtypeStruct((1, 1), F32),
        ),
        in_specs=[vmem] * 3,
        out_specs=(vmem,) * 4,
        scratch_shapes=[
            pltpu.VMEM((high, width), images.dtype),
            pltpu.VMEM((across, width), texts.dtype),
            pltpu.VMEM((high, across), F32),
            pltpu.VMEM((high, across), jnp.bfloat16),
            pltpu.VMEM((gn, 2, high), F32),
            pltpu.VMEM((dn, 2, across), F32),
            pltpu.VMEM((high, wide), F32),
            pltpu.VMEM((rows, wide), F32),
            pltpu.VMEM((1, high), F32),
            pltpu.VMEM((1, across), F32),
            pltpu.VMEM((gn, rows, width), F32),
            pltpu.VMEM((gn, rows, width), F32),
            pltpu.VMEM((dn, rows, width), F32),
            pltpu.VMEM((dn, rows, width), F32),
            pltpu.VMEM((gn, 8, 128), F32),
            pltpu.VMEM((dn, 8, 128), F32),
            pltpu.SemaphoreType.DMA((4, gn)),
            pltpu.SemaphoreType.DMA((4, gn)),
            pltpu.SemaphoreType.DMA((4, dn)),
            pltpu.SemaphoreType.DMA((4, dn)),
        ],
        compiler_params=pltpu.CompilerParams(
            collective_id=0, has_side_effects=True, vmem_limit_bytes=60 * 1024 * 1024),
    )(images, texts, log_scale.reshape(1, 1))
    return gi, gt, loss.reshape(()), scale.reshape(())


def solution(mesh):
    gn, dn = mesh.shape["group"], mesh.shape["dp"]
    spec = P(("dp", "group"), None)
    return jax.shard_map(
        functools.partial(body, gn, dn), mesh=mesh, in_specs=(spec, spec, P()),
        out_specs=(spec, spec, P(), P()), check_vma=False)
```

time: 282 us -> 62.5 us (0.22)
  blocking collectives: 187 us -> 0 us
  Pallas kernels: 0 us -> 55.2 us
  waiting for transfers between devices: 44.8 us -> 0 us
  between operations: 20.3 us -> 4.78 us
  matrix products: 15.1 us -> 0 us
  starting transfers between devices: 7.21 us -> 0 us
  other arithmetic: 5.48 us -> 0 us
    all_gather x3 -> x0, blocking collectives: 149 us -> none  [the longest x1 65.1 us: body(): lax.all_gather(row_lse, ('dp', 'group'), axis=0, tiled=True)]
    pallas_call x0 -> x1, Pallas kernels: none -> 55.2 us  [body(): pl.pallas_call(functools.partial(kernel, gn, dn), out_shape=(jax.ShapeDty...]
    psum x1 -> x0, blocking collectives: 38.4 us -> none  [body(): loss_total, scale_total = lax.psum((loss_part, scale_part), ('dp', 'group'))]
    all_gather x2 -> x0, waiting for transfers between devices: 35 us -> none  [the longest x1 35 us: body(): texts_whole = lax.all_gather(within, 'dp', axis=0, tiled=True)]
    dot_general x3 -> x0, matrix products: 15.1 us -> none  [the longest x1 6.7 us: body(): lax.dot_general(col_grad.astype(jnp.bfloat16), images_whole, contract_fir...]
    all_to_all x2 -> x0, waiting for transfers between devices: 9.04 us -> none  [the longest x1 4.55 us: body(): lax.all_to_all(part_sum.reshape(device_count, row_count), ('dp', 'group')...]
    all_to_all x2 -> x0, starting transfers between devices: 7.13 us -> none  [the longest x1 4.59 us: body(): lax.all_to_all(part_top.reshape(device_count, row_count), ('dp', 'group')...]
    reduce_sum x6 -> x0, other arithmetic: 5.42 us -> none  [the longest x1 2.03 us: body(): jnp.sum(jnp.exp(row_logits - row_top[:, None]), axis=1)]
  transfers between devices with their start and end apart: 4 -> 0, of which waited for: 3 -> 0; matrix products, arithmetic and copies ran while one was open for 5% -> 0% of each run, Pallas kernels for 0% -> 0%
where the time goes in v1:
time: 62.5 us; the launch traced here: 62.3 us
  Pallas kernels  55.2 us (88%)
  between operations  4.78 us (8%)
  local copies, waits for them, and re-layouts  2.26 us (4%)
    pallas_call x1, Pallas kernels, body(): pl.pallas_call(functools.partial(kernel, gn, dn), out_shape=(jax.ShapeDty...  55.2 us
    unnamed x4, local copies, waits for them, and re-layouts  2.26 us

profile of v1, /device:TPU:0, one launch (start us, length us, event | category | flops | bytes accessed | tf_op | source)
XLA Modules:
  0.0 62.3 jit_solution(9275535412894345061)
XLA Ops:
  1.3 55.2 %shard_map.66 = (bf16[128,512]{1,0:T(8,128)(2,1)}, bf16[128,512]{1,0:T(8,128)(2,1)}, f32[1,1]{1,0:T(1,128)}, f32[1,1]{1,0:T(1,128)}) custom-call(bf16[128,512]{1,0:T(8,128)(2,1)} %images.1, bf16[128,512]{1,0:T(8,128)(2,1)} %texts.1, f32[1,1]{1,0:T(1,128)} %bitcast.3.log_scale), custom_call_target="tpu_custom_call" | custom-call | tf_op jit(solution)/shard_map/pallas_call | solution.py:237
  56.5 0.0 copy-start
  56.5 1.6 %copy.12 = bf16[128,512]{1,0:T(8,128)(2,1)} copy(bf16[128,512]{1,0:T(8,128)(2,1)} %get-tuple-element.16) | data formatting | bytes 262144
  58.1 0.0 copy-done
  58.1 0.7 %copy.13 = bf16[128,512]{1,0:T(8,128)(2,1)} copy(bf16[128,512]{1,0:T(8,128)(2,1)S(1)} %copy-done) | data formatting | bytes 262144
Async XLA Ops:
  56.5 1.6 %copy-start = (bf16[128,512]{1,0:T(8,128)(2,1)S(1)}, bf16[128,512]{1,0:T(8,128)(2,1)}, u32[]{:S(2)}) copy-start(bf16[128,512]{1,0:T(8,128)(2,1)} %get-tuple-element.17) | copy-start | bytes 393220

commit v2 on v1

--- a/solution.py
+++ b/solution.py
@@ -13,6 +13,8 @@
 TN = (((0,), (0,)), ((), ()))
 F32 = jnp.float32
 BLOCK, STAT, GRAD, SCALAR = range(4)
+UP, DOWN = range(2)
+PIECES = 2
 
 
 def each(count, step):
@@ -26,7 +28,8 @@
 def kernel(
     gn, dn, images, texts, log_scale, gi_out, gt_out, loss_out, scale_out,
     img_all, txt_all, logits, weights, row_stat, col_stat, top, acc, row_lse, col_lse,
-    gi_send, gi_recv, gt_send, gt_recv, sc_group, sc_dp, g_send, g_recv, d_send, d_recv,
+    gi_send, gi_recv, gt_send, gt_recv, gt_side, sc_group, sc_dp, g_send, g_recv, d_send, d_recv,
+    hop_send, sum_send, sum_recv, side_send, pass_send, side_recv,
 ):
     rows, width = images.shape
     g = lax.axis_index("group")
@@ -35,6 +38,44 @@
     per = wide // rows
     chunks = dn // per
 
+    chip, core = d // per, lax.rem(d, per)
+    side = chip * per + (per - 1 - core)
+    next_g = (lax.min(g + 1, gn - 1), lax.max(g - 1, 0))
+
+    def c_peer(o):
+        return lax.rem(chip + o, chunks)
+
+    def hop(way, k):
+        return pltpu.make_async_remote_copy(
+            src_ref=img_all.at[at(k)], dst_ref=img_all.at[at(k)],
+            send_sem=hop_send.at[way, k], recv_sem=g_recv.at[BLOCK, k],
+            device_id={"group": next_g[way]}, device_id_type=MESH)
+
+    def first_hop(way):
+        return pltpu.make_async_remote_copy(
+            src_ref=images, dst_ref=img_all.at[at(g)],
+            send_sem=hop_send.at[way, g], recv_sem=g_recv.at[BLOCK, g],
+            device_id={"group": next_g[way]}, device_id_type=MESH)
+
+    def sum_hop(way, k, p):
+        piece = pl.ds(p * (rows // PIECES), rows // PIECES)
+        return pltpu.make_async_remote_copy(
+            src_ref=gi_send.at[k, piece], dst_ref=gi_recv.at[way, k, piece],
+            send_sem=sum_send.at[way, k, p], recv_sem=sum_recv.at[way, k, p],
+            device_id={"group": next_g[way]}, device_id_type=MESH)
+
+    def pass_on(k):
+        return pltpu.make_async_remote_copy(
+            src_ref=txt_all.at[at(k)], dst_ref=txt_all.at[at(k)],
+            send_sem=pass_send.at[k], recv_sem=d_recv.at[BLOCK, k],
+            device_id={"dp": side}, device_id_type=MESH)
+
+    def side_copy(c):
+        return pltpu.make_async_remote_copy(
+            src_ref=gt_send.at[c * per + (per - 1 - core)], dst_ref=gt_side.at[c],
+            send_sem=side_send.at[c], recv_sem=side_recv.at[c],
+            device_id={"dp": side}, device_id_type=MESH)
+
     def g_peer(o):
         return lax.rem(g + o, gn)
 
@@ -61,31 +102,61 @@
         barrier, inc=1, device_id={"dp": d_peer(i + 1)}, device_id_type=MESH))
     pl.semaphore_wait(barrier, gn + dn - 2)
 
-    each(gn - 1, lambda i: g_copy(BLOCK, images, img_all.at[at(g)], g_peer(i + 1), g).start())
-    each(dn - 1, lambda i: d_copy(BLOCK, texts, txt_all.at[at(d)], d_peer(i + 1), d).start())
+    def text_block(k):
+        return d_copy(BLOCK, texts, txt_all.at[at(d)], k, d)
+
+    @pl.when(g < gn - 1)
+    def _():
+        first_hop(UP).start()
+
+    @pl.when(g > 0)
+    def _():
+        first_hop(DOWN).start()
+
+    each(chunks - 1, lambda i: text_block(c_peer(i + 1) * per + core).start())
+    if per == 2:
+        text_block(side).start()
     img_all[at(g), :] = images[...]
     txt_all[at(d), :] = texts[...]
     s = jnp.exp(log_scale[...])
     eye = (lax.broadcasted_iota(jnp.int32, (rows, rows), 0)
            == lax.broadcasted_iota(jnp.int32, (rows, rows), 1))
 
-    def wait_image(i):
-        k = g_peer(i + 1)
-        g_copy(BLOCK, images, img_all.at[at(k)], k, k).wait_recv()
-
-    each(gn - 1, wait_image)
+    def relay_images(j):
+        @pl.when(g - j >= 0)
+        def _():
+            hop(UP, g - j).wait_recv()
+
+            @pl.when(g < gn - 1)
+            def _():
+                hop(UP, g - j).start()
+
+        @pl.when(g + j < gn)
+        def _():
+            hop(DOWN, g + j).wait_recv()
+
+            @pl.when(g > 0)
+            def _():
+                hop(DOWN, g + j).start()
+
+    def relay_text(i):
+        k = c_peer(i + 1) * per + core
+        d_copy(BLOCK, texts, txt_all.at[at(k)], k, k).wait_recv()
+        if per == 2:
+            pass_on(k).start()
+
+    for j in range(1, gn):
+        relay_images(j)
+        if j == 1:
+            each(chunks - 1, relay_text)
+    if gn == 1:
+        each(chunks - 1, relay_text)
 
     def logits_chunk(i):
-        c = lax.rem(d // per + i, chunks)
-
-        def wait_text(j):
-            k = c * per + j
-
-            @pl.when(k != d)
-            def _():
-                d_copy(BLOCK, texts, txt_all.at[at(k)], k, k).wait_recv()
-
-        each(per, wait_text)
+        c = c_peer(i)
+        if per == 2:
+            k = c * per + (per - 1 - core)
+            d_copy(BLOCK, texts, txt_all.at[at(k)], k, k).wait_recv()
         part = s * lax.dot_general(img_all[...], txt_all[at(c, wide), :], NT, preferred_element_type=F32)
         logits[:, at(c, wide)] = part
         high = jnp.max(part, axis=0, keepdims=True)
@@ -138,24 +209,31 @@
     row_lse[...] = lse(row_stat)
 
     acc[...] = jnp.zeros(acc.shape, F32)
+    across = 4 * dn * rows
     step_of = (lax.broadcasted_iota(jnp.int32, (rows, wide), 1)
                - lax.broadcasted_iota(jnp.int32, (rows, wide), 0))
-    for o in [*range(1, gn), 0]:
-        k = g_peer(o)
+    order = sorted(range(gn), key=lambda t: (-abs(2 * t - gn + 1), -t))
+    for k in order:
         line = stand(row_lse[0:1, at(k)])
 
         def weigh(c):
             part = logits[at(k), at(c, wide)]
             w = 0.5 * (jnp.exp(part - line) + jnp.exp(part - col_lse[0:1, at(c, wide)]))
-            if o == 0:
-                w = w - jnp.where(step_of == d * rows - c * wide, 1.0, 0.0)
+            w = w - jnp.where(step_of == jnp.where(k == g, d * rows - c * wide, -across), 1.0, 0.0)
             acc[...] += w * part
             weights[at(k), at(c, wide)] = w.astype(jnp.bfloat16)
 
         each(chunks, weigh)
         gi_send[k] = lax.dot_general(weights[at(k), :], txt_all[...], NN, preferred_element_type=F32)
-        if o:
-            g_copy(GRAD, gi_send.at[k], gi_recv.at[g], k, g).start()
+        for p in range(PIECES):
+            if k > 0:
+                @pl.when(g == 0)
+                def _():
+                    sum_hop(UP, k, p).start()
+            if k < gn - 1:
+                @pl.when(g == gn - 1)
+                def _():
+                    sum_hop(DOWN, k, p).start()
 
     own = logits[at(g), at(d)]
     pairs = jnp.sum(jnp.where(eye, own, 0.0), axis=0, keepdims=True)
@@ -165,18 +243,54 @@
     sc_group[g] = jnp.where(first, loss_part, scale_part)
     each(gn - 1, lambda i: g_copy(SCALAR, sc_group.at[g], sc_group.at[g], g_peer(i + 1), g).start())
 
+    def share(i):
+        c = c_peer(1 + i)
+        k = c * per + core
+        if per == 2:
+            side_copy(c).wait_recv()
+            gt_send[k] += gt_side[c]
+
+        @pl.when(c != chip)
+        def _():
+            pltpu.make_async_remote_copy(
+                src_ref=gt_send.at[k], dst_ref=gt_recv.at[chip],
+                send_sem=d_send.at[GRAD, c], recv_sem=d_recv.at[GRAD, chip],
+                device_id={"dp": k}, device_id_type=MESH).start()
+
     def text_chunk(i):
-        c = lax.rem(d // per + 1 + i, chunks)
+        c = c_peer(1 + i)
         part = lax.dot_general(weights[:, at(c, wide)], img_all[...], TN, preferred_element_type=F32)
         for j in range(per):
-            k = c * per + j
-            gt_send[k] = part[j * rows:(j + 1) * rows]
-
-            @pl.when(k != d)
-            def _():
-                d_copy(GRAD, gt_send.at[k], gt_recv.at[d], k, d).start()
+            gt_send[c * per + j] = part[j * rows:(j + 1) * rows]
+        if per == 2:
+            side_copy(c).start()
+        if isinstance(i, int):
+            if i > 0:
+                share(i - 1)
+        else:
+            @pl.when(i > 0)
+            def _():
+                share(i - 1)
 
     each(chunks, text_chunk)
+    share(chunks - 1)
+
+    def add_sum(way, k, p):
+        piece = pl.ds(p * (rows // PIECES), rows // PIECES)
+        sum_hop(way, k, p).wait_recv()
+        gi_send[k, piece] += gi_recv[way, k, piece]
+
+    for j in range(gn - 1):
+        for p in range(PIECES):
+            @pl.when((g > 0) & (gn - 1 - j > g))
+            def _():
+                add_sum(UP, gn - 1 - j, p)
+                sum_hop(UP, gn - 1 - j, p).start()
+
+            @pl.when((g < gn - 1) & (j < g))
+            def _():
+                add_sum(DOWN, j, p)
+                sum_hop(DOWN, j, p).start()
 
     def wait_sc_group(i):
         k = g_peer(i + 1)
@@ -186,20 +300,27 @@
     sc_dp[d] = jnp.sum(sc_group[...], axis=0)
     each(dn - 1, lambda i: d_copy(SCALAR, sc_dp.at[d], sc_dp.at[d], d_peer(i + 1), d).start())
 
-    def take_g(i):
-        k = g_peer(i + 1)
-        g_copy(GRAD, gi_send.at[k], gi_recv.at[k], k, k).wait_recv()
-        gi_send[g] += gi_recv[k]
-
     def take_d(i):
-        k = d_peer(i + 1)
-        d_copy(GRAD, gt_send.at[k], gt_recv.at[k], k, k).wait_recv()
-        gt_send[d] += gt_recv[k]
-
-    each(gn - 1, take_g)
+        c = c_peer(i + 1)
+        pltpu.make_async_remote_copy(
+            src_ref=gt_recv.at[c], dst_ref=gt_recv.at[c],
+            send_sem=d_send.at[GRAD, c], recv_sem=d_recv.at[GRAD, c],
+            device_id={"dp": c * per + core}, device_id_type=MESH).wait_recv()
+        gt_send[d] += gt_recv[c]
+
+    each(chunks - 1, take_d)
+    gt_out[...] = (s * gt_send[d]).astype(gt_out.dtype)
+
+    for p in range(PIECES):
+        @pl.when(g > 0)
+        def _():
+            add_sum(UP, g, p)
+
+        @pl.when(g < gn - 1)
+        def _():
+            add_sum(DOWN, g, p)
+
     gi_out[...] = (s * gi_send[g]).astype(gi_out.dtype)
-    each(dn - 1, take_d)
-    gt_out[...] = (s * gt_send[d]).astype(gt_out.dtype)
 
     def wait_sc_dp(i):
         k = d_peer(i + 1)
@@ -213,26 +334,57 @@
 
     def end_g(i):
         k = g_peer(i + 1)
-        g_copy(BLOCK, images, img_all.at[at(g)], k, g).wait_send()
         g_copy(STAT, row_stat.at[g], row_stat.at[g], k, g).wait_send()
-        g_copy(GRAD, gi_send.at[k], gi_recv.at[g], k, g).wait_send()
         g_copy(SCALAR, sc_group.at[g], sc_group.at[g], k, g).wait_send()
 
     def end_d(i):
         k = d_peer(i + 1)
-        d_copy(BLOCK, texts, txt_all.at[at(d)], k, d).wait_send()
         d_copy(STAT, col_stat.at[d], col_stat.at[d], k, d).wait_send()
-        d_copy(GRAD, gt_send.at[k], gt_recv.at[d], k, d).wait_send()
         d_copy(SCALAR, sc_dp.at[d], sc_dp.at[d], k, d).wait_send()
+
+    def end_c(i):
+        c = c_peer(i + 1)
+        k = c * per + core
+        text_block(k).wait_send()
+        if per == 2:
+            pass_on(k).wait_send()
+            side_copy(c).wait_send()
+        pltpu.make_async_remote_copy(
+            src_ref=gt_send.at[k], dst_ref=gt_recv.at[chip],
+            send_sem=d_send.at[GRAD, c], recv_sem=d_recv.at[GRAD, chip],
+            device_id={"dp": k}, device_id_type=MESH).wait_send()
 
     each(gn - 1, end_g)
     each(dn - 1, end_d)
+    each(chunks - 1, end_c)
+    if per == 2:
+        text_block(side).wait_send()
+        side_copy(chip).wait_send()
+
+    for k in range(gn):
+        @pl.when((g < gn - 1) & (k <= g))
+        def _():
+            hop(UP, k).wait_send()
+
+        @pl.when((g > 0) & (k >= g))
+        def _():
+            hop(DOWN, k).wait_send()
+
+        for p in range(PIECES):
+            @pl.when(k > g)
+            def _():
+                sum_hop(UP, k, p).wait_send()
+
+            @pl.when(k < g)
+            def _():
+                sum_hop(DOWN, k, p).wait_send()
 
 
 def body(gn, dn, images, texts, log_scale):
     rows, width = images.shape
     high, across = gn * rows, dn * rows
     wide = 2 * rows if dn % 2 == 0 else rows
+    chunks = across // wide
     vmem = pl.BlockSpec(memory_space=pltpu.VMEM)
     gi, gt, loss, scale = pl.pallas_call(
         functools.partial(kernel, gn, dn),
@@ -256,15 +408,22 @@
             pltpu.VMEM((1, high), F32),
             pltpu.VMEM((1, across), F32),
             pltpu.VMEM((gn, rows, width), F32),
-            pltpu.VMEM((gn, rows, width), F32),
+            pltpu.VMEM((2, gn, rows, width), F32),
             pltpu.VMEM((dn, rows, width), F32),
-            pltpu.VMEM((dn, rows, width), F32),
+            pltpu.VMEM((chunks, rows, width), F32),
+            pltpu.VMEM((chunks, rows, width), F32),
             pltpu.VMEM((gn, 8, 128), F32),
             pltpu.VMEM((dn, 8, 128), F32),
             pltpu.SemaphoreType.DMA((4, gn)),
             pltpu.SemaphoreType.DMA((4, gn)),
             pltpu.SemaphoreType.DMA((4, dn)),
             pltpu.SemaphoreType.DMA((4, dn)),
+            pltpu.SemaphoreType.DMA((2, gn)),
+            pltpu.SemaphoreType.DMA((2, gn, PIECES)),
+            pltpu.SemaphoreType.DMA((2, gn, PIECES)),
+            pltpu.SemaphoreType.DMA((chunks,)),
+            pltpu.SemaphoreType.DMA((dn,)),
+            pltpu.SemaphoreType.DMA((chunks,)),
         ],
         compiler_params=pltpu.CompilerParams(
             collective_id=0, has_side_effects=True, vmem_limit_bytes=60 * 1024 * 1024),

time: 62.5 us -> 61.8 us (0.989)
  Pallas kernels: 55.2 us -> 54.5 us
    pallas_call x1, Pallas kernels: 55.2 us -> 54.5 us  [body(): pl.pallas_call(functools.partial(kernel, gn, dn), out_shape=(jax.ShapeDty...]
where the time goes in v2:
time: 61.8 us; the launch traced here: 61.6 us
  Pallas kernels  54.5 us (88%)
  between operations  4.78 us (8%)
  local copies, waits for them, and re-layouts  2.26 us (4%)
    pallas_call x1, Pallas kernels, body(): pl.pallas_call(functools.partial(kernel, gn, dn), out_shape=(jax.ShapeDty...  54.5 us
    unnamed x4, local copies, waits for them, and re-layouts  2.26 us

profile of v2, /device:TPU:0, one launch (start us, length us, event | category | flops | bytes accessed | tf_op | source)
XLA Modules:
  0.0 61.6 jit_solution(5547492251595567753)
XLA Ops:
  1.3 54.5 %shard_map.66 = (bf16[128,512]{1,0:T(8,128)(2,1)}, bf16[128,512]{1,0:T(8,128)(2,1)}, f32[1,1]{1,0:T(1,128)}, f32[1,1]{1,0:T(1,128)}) custom-call(bf16[128,512]{1,0:T(8,128)(2,1)} %images.1, bf16[128,512]{1,0:T(8,128)(2,1)} %texts.1, f32[1,1]{1,0:T(1,128)} %bitcast.3.log_scale), custom_call_target="tpu_custom_call" | custom-call | tf_op jit(solution)/shard_map/pallas_call | solution.py:389
  55.8 0.0 copy-start
  55.8 1.6 %copy.12 = bf16[128,512]{1,0:T(8,128)(2,1)} copy(bf16[128,512]{1,0:T(8,128)(2,1)} %get-tuple-element.16) | data formatting | bytes 262144
  57.4 0.0 copy-done
  57.4 0.7 %copy.13 = bf16[128,512]{1,0:T(8,128)(2,1)} copy(bf16[128,512]{1,0:T(8,128)(2,1)S(1)} %copy-done) | data formatting | bytes 262144
Async XLA Ops:
  55.8 1.6 %copy-start = (bf16[128,512]{1,0:T(8,128)(2,1)S(1)}, bf16[128,512]{1,0:T(8,128)(2,1)}, u32[]{:S(2)}) copy-start(bf16[128,512]{1,0:T(8,128)(2,1)} %get-tuple-element.17) | copy-start | bytes 393220

commit v3 on v2

--- a/solution.py
+++ b/solution.py
@@ -14,7 +14,7 @@
 F32 = jnp.float32
 BLOCK, STAT, GRAD, SCALAR = range(4)
 UP, DOWN = range(2)
-PIECES = 2
+PIECES = 1
 
 
 def each(count, step):
@@ -145,50 +145,70 @@
         if per == 2:
             pass_on(k).start()
 
-    for j in range(1, gn):
+    def flat(col):
+        return jnp.sum(jnp.where(eye, col, 0.0), axis=0, keepdims=True)
+
+    def stand(line):
+        return jnp.sum(jnp.where(eye, line, 0.0), axis=1, keepdims=True)
+
+    def wait_side(i):
+        k = c_peer(i) * per + (per - 1 - core)
+        d_copy(BLOCK, texts, txt_all.at[at(k)], k, k).wait_recv()
+
+    def band_logits(k, first=False):
+        top[...] = jnp.full(top.shape, -jnp.inf, F32)
+        acc[...] = jnp.zeros(acc.shape, F32)
+
+        def fill(c):
+            cols = at(c, wide)
+            part = s * lax.dot_general(img_all[at(k), :], txt_all[cols, :], NT, preferred_element_type=F32)
+            logits[at(k), cols] = part
+            top[...] = jnp.maximum(top[...], part)
+            peak = jnp.max(part, axis=0, keepdims=True)
+            if first:
+                col_stat[d, 0:1, cols] = peak
+                col_stat[d, 1:2, cols] = jnp.sum(jnp.exp(part - peak), axis=0, keepdims=True)
+            else:
+                old = col_stat[d, 0:1, cols]
+                peak = jnp.maximum(old, peak)
+                col_stat[d, 0:1, cols] = peak
+                col_stat[d, 1:2, cols] = (col_stat[d, 1:2, cols] * jnp.exp(old - peak)
+                                          + jnp.sum(jnp.exp(part - peak), axis=0, keepdims=True))
+
+        each(chunks, fill)
+        high = jnp.max(top[...], axis=1, keepdims=True)
+
+        def add(c):
+            acc[...] += jnp.exp(logits[at(k), at(c, wide)] - high)
+
+        each(chunks, add)
+        row_stat[g, 0:1, at(k)] = flat(high)
+        row_stat[g, 1:2, at(k)] = flat(jnp.sum(acc[...], axis=1, keepdims=True))
+
+    def both_bands(j):
+        @pl.when(g - j >= 0)
+        def _():
+            band_logits(g - j)
+
+        @pl.when(g + j < gn)
+        def _():
+            band_logits(g + j)
+
+    for j in range(1, gn - 1):
         relay_images(j)
         if j == 1:
             each(chunks - 1, relay_text)
-    if gn == 1:
+    if gn <= 2:
         each(chunks - 1, relay_text)
-
-    def logits_chunk(i):
-        c = c_peer(i)
-        if per == 2:
-            k = c * per + (per - 1 - core)
-            d_copy(BLOCK, texts, txt_all.at[at(k)], k, k).wait_recv()
-        part = s * lax.dot_general(img_all[...], txt_all[at(c, wide), :], NT, preferred_element_type=F32)
-        logits[:, at(c, wide)] = part
-        high = jnp.max(part, axis=0, keepdims=True)
-        col_stat[d, 0:1, at(c, wide)] = high
-        col_stat[d, 1:2, at(c, wide)] = jnp.sum(jnp.exp(part - high), axis=0, keepdims=True)
-        if isinstance(i, int) and i == 0:
-            top[...] = part
-        else:
-            top[...] = jnp.maximum(top[...], part)
-
-    if chunks > 8:
-        top[...] = jnp.full(top.shape, -jnp.inf, F32)
-    each(chunks, logits_chunk)
+    if per == 2:
+        each(chunks, wait_side)
+    band_logits(g, True)
+    for j in range(1, gn - 1):
+        both_bands(j)
+    if gn > 1:
+        relay_images(gn - 1)
+        both_bands(gn - 1)
     each(dn - 1, lambda i: d_copy(STAT, col_stat.at[d], col_stat.at[d], d_peer(i + 1), d).start())
-
-    def flat(col):
-        return jnp.sum(jnp.where(eye, col, 0.0), axis=0, keepdims=True)
-
-    def stand(line):
-        return jnp.sum(jnp.where(eye, line, 0.0), axis=1, keepdims=True)
-
-    for k in range(gn):
-        band = pl.ds(k * rows, rows)
-        high = jnp.max(top[band, :], axis=1, keepdims=True)
-        acc[...] = jnp.zeros(acc.shape, F32)
-
-        def add(c):
-            acc[...] += jnp.exp(logits[band, at(c, wide)] - high)
-
-        each(chunks, add)
-        row_stat[g, 0:1, band] = flat(high)
-        row_stat[g, 1:2, band] = flat(jnp.sum(acc[...], axis=1, keepdims=True))
     each(gn - 1, lambda i: g_copy(STAT, row_stat.at[g], row_stat.at[g], g_peer(i + 1), g).start())
 
     def wait_row(i):
@@ -213,7 +233,9 @@
     step_of = (lax.broadcasted_iota(jnp.int32, (rows, wide), 1)
                - lax.broadcasted_iota(jnp.int32, (rows, wide), 0))
     order = sorted(range(gn), key=lambda t: (-abs(2 * t - gn + 1), -t))
-    for k in order:
+
+
+    def weigh_band(k):
         line = stand(row_lse[0:1, at(k)])
 
         def weigh(c):
@@ -224,6 +246,8 @@
             weights[at(k), at(c, wide)] = w.astype(jnp.bfloat16)
 
         each(chunks, weigh)
+
+    def give(k):
         gi_send[k] = lax.dot_general(weights[at(k), :], txt_all[...], NN, preferred_element_type=F32)
         for p in range(PIECES):
             if k > 0:
@@ -235,6 +259,12 @@
                 def _():
                     sum_hop(DOWN, k, p).start()
 
+    for k in order[:2]:
+        weigh_band(k)
+        give(k)
+    for k in order[2:]:
+        weigh_band(k)
+
     own = logits[at(g), at(d)]
     pairs = jnp.sum(jnp.where(eye, own, 0.0), axis=0, keepdims=True)
     loss_part = jnp.sum(row_lse[0:1, at(g)] + col_lse[0:1, at(d)] - 2.0 * pairs, axis=1, keepdims=True)
@@ -242,6 +272,9 @@
     first = lax.broadcasted_iota(jnp.int32, (8, 128), 1) == 0
     sc_group[g] = jnp.where(first, loss_part, scale_part)
     each(gn - 1, lambda i: g_copy(SCALAR, sc_group.at[g], sc_group.at[g], g_peer(i + 1), g).start())
+
+    for k in order[2:]:
+        give(k)
 
     def share(i):
         c = c_peer(1 + i)
@@ -280,6 +313,17 @@
         sum_hop(way, k, p).wait_recv()
         gi_send[k, piece] += gi_recv[way, k, piece]
 
+    def wait_sc_group(i):
+        k = g_peer(i + 1)
+        g_copy(SCALAR, sc_group.at[k], sc_group.at[k], k, k).wait_recv()
+
+    def pass_scalars():
+        each(gn - 1, wait_sc_group)
+        sc_dp[d] = jnp.sum(sc_group[...], axis=0)
+        each(dn - 1, lambda i: d_copy(SCALAR, sc_dp.at[d], sc_dp.at[d], d_peer(i + 1), d).start())
+
+    if gn == 1:
+        pass_scalars()
     for j in range(gn - 1):
         for p in range(PIECES):
             @pl.when((g > 0) & (gn - 1 - j > g))
@@ -292,13 +336,8 @@
                 add_sum(DOWN, j, p)
                 sum_hop(DOWN, j, p).start()
 
-    def wait_sc_group(i):
-        k = g_peer(i + 1)
-        g_copy(SCALAR, sc_group.at[k], sc_group.at[k], k, k).wait_recv()
-
-    each(gn - 1, wait_sc_group)
-    sc_dp[d] = jnp.sum(sc_group[...], axis=0)
-    each(dn - 1, lambda i: d_copy(SCALAR, sc_dp.at[d], sc_dp.at[d], d_peer(i + 1), d).start())
+        if j == 0:
+            pass_scalars()
 
     def take_d(i):
         c = c_peer(i + 1)
@@ -403,7 +442,7 @@
             pltpu.VMEM((high, across), jnp.bfloat16),
             pltpu.VMEM((gn, 2, high), F32),
             pltpu.VMEM((dn, 2, across), F32),
-            pltpu.VMEM((high, wide), F32),
+            pltpu.VMEM((rows, wide), F32),
             pltpu.VMEM((rows, wide), F32),
             pltpu.VMEM((1, high), F32),
             pltpu.VMEM((1, across), F32),

time: 61.8 us -> 58.7 us (0.950)
  Pallas kernels: 54.5 us -> 51.3 us
    pallas_call x1, Pallas kernels: 54.5 us -> 51.3 us  [body(): pl.pallas_call(functools.partial(kernel, gn, dn), out_shape=(jax.ShapeDty...]
where the time goes in v3:
time: 58.7 us; the launch traced here: 58.4 us
  Pallas kernels  51.3 us (87%)
  between operations  4.78 us (8%)
  local copies, waits for them, and re-layouts  2.26 us (4%)
    pallas_call x1, Pallas kernels, body(): pl.pallas_call(functools.partial(kernel, gn, dn), out_shape=(jax.ShapeDty...  51.3 us
    unnamed x4, local copies, waits for them, and re-layouts  2.26 us

profile of v3, /device:TPU:0, one launch (start us, length us, event | category | flops | bytes accessed | tf_op | source)
XLA Modules:
  0.0 58.4 jit_solution(14110568536671427412)
XLA Ops:
  1.3 51.3 %shard_map.66 = (bf16[128,512]{1,0:T(8,128)(2,1)}, bf16[128,512]{1,0:T(8,128)(2,1)}, f32[1,1]{1,0:T(1,128)}, f32[1,1]{1,0:T(1,128)}) custom-call(bf16[128,512]{1,0:T(8,128)(2,1)} %images.1, bf16[128,512]{1,0:T(8,128)(2,1)} %texts.1, f32[1,1]{1,0:T(1,128)} %bitcast.3.log_scale), custom_call_target="tpu_custom_call" | custom-call | tf_op jit(solution)/shard_map/pallas_call | solution.py:428
  52.6 0.0 copy-start
  52.6 1.6 %copy.12 = bf16[128,512]{1,0:T(8,128)(2,1)} copy(bf16[128,512]{1,0:T(8,128)(2,1)} %get-tuple-element.16) | data formatting | bytes 262144
  54.2 0.0 copy-done
  54.2 0.7 %copy.13 = bf16[128,512]{1,0:T(8,128)(2,1)} copy(bf16[128,512]{1,0:T(8,128)(2,1)S(1)} %copy-done) | data formatting | bytes 262144
Async XLA Ops:
  52.6 1.6 %copy-start = (bf16[128,512]{1,0:T(8,128)(2,1)S(1)}, bf16[128,512]{1,0:T(8,128)(2,1)}, u32[]{:S(2)}) copy-start(bf16[128,512]{1,0:T(8,128)(2,1)} %get-tuple-element.17) | copy-start | bytes 393220
